TPU v7x, 32 devices: a whole 2x2x4 slice. The times are simulated.
32 devices in a mesh: seq: 16 (over z, x, core), tp: 2 (over y).
Axes of the slice: x: 2, y: 2, z: 4, core: 2. Of those that a mesh axis runs over, the one named last changes fastest.
Arguments:
- tokens: bfloat16 [4096, 4096], P('seq', 'tp'), may hold values from -6 to 6
- decay_rate: float32 [4096, 16], P('tp'), as said below
- angle: float32 [4096, 16], P('tp'), may hold values from -3.140625 to 3.140625
- in_coef: float32 [4096, 16], P('tp'), may hold values from -4 to 4
- out_coef: float32 [2, 4096, 16], P(None, 'tp'), may hold values from -1.5 to 1.5
- skip_coef: float32 [4096], P('tp'), may hold values from 0.3 to 1.5
- gate_weight: bfloat16 [4096, 4096], P('seq', 'tp'), may hold values from -0.09375 to 0.09375
- out_weight: bfloat16 [4096, 4096], P('seq', 'tp'), may hold values from -0.09375 to 0.09375
Outputs:
- mixed_out: bfloat16 [4096, 4096], P('seq', 'tp')
Inputs may be any that keep to these rules, and one draw needn't show every extreme that they name: `decay_rate`: every entry is positive and below 0.034.
All inputs are finite; a program needn't handle non-finite values.
Results may differ from a plain program's by a relative error of at most 0.01.
Values may be sent and summed in bfloat16 or wider, within the bound.
A program may use at most 192 MiB of HBM per device.

v0:
```python
import jax
import jax.numpy as jnp
import numpy as np
from jax import lax
from jax.sharding import PartitionSpec as P

BLOCK = 32


def powers(log_mag, angle, exponents):
    scaled_log = exponents[:, None, None] * log_mag
    damping = jnp.exp(scaled_log)
    rotation = exponents[:, None, None] * angle
    return (damping * jnp.cos(rotation), damping * jnp.sin(rotation))


def complex_mul(left_re, left_im, right_re, right_im):
    return (left_re * right_re - left_im * right_im, left_re * right_im + left_im * right_re)


def split_einsum(form, data, table):
    upper = table.astype(jnp.bfloat16)
    lower = (table - upper.astype(jnp.float32)).astype(jnp.bfloat16)
    first = jnp.einsum(form, data, upper, preferred_element_type=jnp.float32)
    return first + jnp.einsum(form, data, lower, preferred_element_type=jnp.float32)


def per_device(tokens, decay_rate, angle, in_coef, out_coef, skip_coef, gate_weight, out_weight):
    tok_rows, channels = tokens.shape
    blocks = tok_rows // BLOCK
    values = tokens.astype(jnp.float32)
    log_mag = jnp.log1p(-decay_rate)
    magnitude = 1.0 - decay_rate
    scaled = in_coef * jnp.sqrt(1.0 - magnitude * magnitude)
    out_re = out_coef[0]
    out_im = out_coef[1]
    highest = lax.Precision.HIGHEST
    offsets = jnp.arange(BLOCK).astype(jnp.float32)
    pow_re, pow_im = powers(log_mag, angle, offsets)
    kernel = jnp.sum(scaled * (out_re * pow_re - out_im * pow_im), axis=2)
    gap_table = np.arange(BLOCK)[:, None] - np.arange(BLOCK)[None, :]
    lag_index = np.clip(gap_table, 0, None)
    causal = jnp.asarray(gap_table >= 0)
    toeplitz = jnp.where(causal[:, :, None], kernel[lag_index], 0.0)
    shaped = tokens.reshape(blocks, BLOCK, channels)
    within = split_einsum("bsc,tsc->btc", shaped, toeplitz)
    back_re, back_im = powers(log_mag, angle, BLOCK - 1 - offsets)
    inject_re = split_einsum("bsc,sch->bch", shaped, back_re * scaled)
    inject_im = split_einsum("bsc,sch->bch", shaped, back_im * scaled)
    next_re, next_im = powers(log_mag, angle, offsets + 1.0)
    read_re, read_im = complex_mul(out_re, out_im, next_re, next_im)
    step_re, step_im = powers(log_mag, angle, jnp.full((1,), BLOCK, jnp.float32))
    step_re = step_re[0]
    step_im = step_im[0]

    def advance(current, inject):
        new_re, new_im = complex_mul(step_re, step_im, current[0], current[1])
        return ((new_re + inject[0], new_im + inject[1]), current)

    empty_state = jnp.zeros(decay_rate.shape, jnp.float32)
    (local_re, local_im), (before_re, before_im) = lax.scan(
        advance, (empty_state, empty_state), (inject_re, inject_im)
    )
    span_re, span_im = powers(log_mag, angle, jnp.full((1,), tok_rows, jnp.float32))
    span_re = span_re[0]
    span_im = span_im[0]
    all_re, all_im = (
        lax.all_gather(local_re[None].astype(jnp.bfloat16), "seq", axis=0, tiled=True).astype(
            jnp.float32
        ),
        lax.all_gather(local_im[None].astype(jnp.bfloat16), "seq", axis=0, tiled=True).astype(
            jnp.float32
        ),
    )
    position = lax.axis_index("seq")

    def horner(current, element):
        index_k, piece_re, piece_im = element
        new_re, new_im = complex_mul(span_re, span_im, current[0], current[1])
        keeps = index_k < position
        return (
            (
                jnp.where(keeps, new_re + piece_re, current[0]),
                jnp.where(keeps, new_im + piece_im, current[1]),
            ),
            None,
        )

    counts = jnp.arange(all_re.shape[0], dtype=jnp.int32)
    (enter_re, enter_im), unused = lax.scan(
        horner, (empty_state, empty_state), (counts, all_re, all_im)
    )
    block_starts = jnp.arange(blocks).astype(jnp.float32) * BLOCK
    carry_re, carry_im = powers(log_mag, angle, block_starts)
    moved_re, moved_im = complex_mul(carry_re, carry_im, enter_re[None], enter_im[None])
    total_re = before_re + moved_re
    total_im = before_im + moved_im
    from_state = jnp.einsum("jch,bch->bjc", read_re, total_re, precision=highest) - jnp.einsum(
        "jch,bch->bjc", read_im, total_im, precision=highest
    )
    smoothed = (within + from_state).reshape(tok_rows, channels) + skip_coef * values
    features_all = lax.all_gather(tokens, "tp", axis=1, tiled=True)
    columns = features_all
    gate_pre = jnp.dot(
        columns,
        lax.all_gather(gate_weight, "seq", axis=0, tiled=True),
        preferred_element_type=jnp.float32,
    )
    hidden = (jax.nn.silu(smoothed) * jax.nn.sigmoid(gate_pre)).astype(jnp.bfloat16)
    hidden_all = lax.all_gather(hidden, "tp", axis=1, tiled=True)
    columns = hidden_all
    mixed_out = jnp.dot(
        columns,
        lax.all_gather(out_weight, "seq", axis=0, tiled=True),
        preferred_element_type=jnp.float32,
    )
    return mixed_out.astype(jnp.bfloat16)


def solution(mesh):
    in_specs = (
        P("seq", "tp"),
        P("tp", None),
        P("tp", None),
        P("tp", None),
        P(None, "tp", None),
        P("tp"),
        P("seq", "tp"),
        P("seq", "tp"),
    )
    out_specs = P("seq", "tp")
    return jax.shard_map(
        per_device, mesh=mesh, in_specs=in_specs, out_specs=out_specs, check_vma=False
    )
```

profile of v0, /device:TPU:0, one launch (start us, length us, event | category | flops | bytes accessed | tf_op | source)
XLA Modules:
  0.0 612.4 jit_solution(5681265062917030125)
XLA Ops:
  7.6 2.0 sine_multiply_fusion
  9.6 54.2 %subtract_convert_fusion.2 = (bf16[32,2048,16]{1,2,0:T(8,128)(2,1)}, bf16[32,2048,16]{1,2,0:T(8,128)(2,1)}, bf16[32,2048,16]{1,2,0:T(8,128)(2,1)}, bf16[32,2048,...) fusion(f32[32]{0:T(128)S(1)} %get-tuple-element.297, ...), kind=kLoop, calls=%fused_computation.46 | loop fusion | flops 34537472 | bytes 17695104 | tf_op jit(solution)/shard_map/convert_element_type | solution.py:23
  63.8 13.0 %copy.77 = bf16[32,2048,16]{0,2,1:T(8,128)(2,1)} copy(bf16[32,2048,16]{1,2,0:T(8,128)(2,1)} %get-tuple-element.284) | data formatting | bytes 4194304 | tf_op jit(solution)/shard_map/convert_element_type | solution.py:22
  76.8 4.2 copy.71
  81.0 13.0 %copy.79 = bf16[32,2048,16]{0,2,1:T(8,128)(2,1)} copy(bf16[32,2048,16]{1,2,0:T(8,128)(2,1)} %get-tuple-element.281) | data formatting | bytes 4194304 | tf_op jit(solution)/shard_map/convert_element_type | solution.py:23
  94.0 12.3 %fusion.35 = f32[2048,16,8]{1,2,0:T(8,128)} fusion(bf16[32,2048,16]{0,2,1:T(8,128)(2,1)} %copy.77, bf16[8,32,2048]{1,0,2:T(8,128)(2,1)} %copy.71), kind=kOutput, calls=%fused_computation.84 | convolution fusion | flops 16777216 | bytes 4194304 | tf_op jit(solution)/shard_map/bsc,sch->bch/dot_general | solution.py:24
  106.3 14.8 %add_bitcast_fusion = f32[8,2048,16]{2,0,1:T(8,128)} fusion(f32[2048,16,8]{1,2,0:T(8,128)} %fusion.35, bf16[32,2048,16]{0,2,1:T(8,128)(2,1)} %copy.79, bf16[8,32,2048]{1,0,2:T(8,128)(2,1)} %copy.71), kind=kOutput, calls=%fused_computation.22 | convolution fusion | flops 17039360 | bytes 5242880 | tf_op jit(solution)/shard_map/bsc,sch->bch/dot_general | solution.py:25
  121.0 5.1 copy.82
  126.2 13.2 %copy.73 = bf16[32,2048,16]{0,2,1:T(8,128)(2,1)} copy(bf16[32,2048,16]{1,2,0:T(8,128)(2,1)} %get-tuple-element.282) | data formatting | bytes 4194304 | tf_op jit(solution)/shard_map/convert_element_type | solution.py:22
  139.4 12.3 %fusion.34 = f32[2048,16,8]{1,2,0:T(8,128)} fusion(bf16[32,2048,16]{0,2,1:T(8,128)(2,1)} %copy.73, bf16[8,32,2048]{1,0,2:T(8,128)(2,1)} %copy.71), kind=kOutput, calls=%fused_computation.83 | convolution fusion | flops 16777216 | bytes 4194304 | tf_op jit(solution)/shard_map/bsc,sch->bch/dot_general | solution.py:24
  151.7 12.8 %copy.75 = bf16[32,2048,16]{0,2,1:T(8,128)(2,1)} copy(bf16[32,2048,16]{1,2,0:T(8,128)(2,1)} %get-tuple-element.283) | data formatting | bytes 4194304 | tf_op jit(solution)/shard_map/convert_element_type | solution.py:23
  164.5 14.8 %add_bitcast_fusion.1 = f32[8,2048,16]{2,0,1:T(8,128)} fusion(f32[2048,16,8]{1,2,0:T(8,128)} %fusion.34, bf16[32,2048,16]{0,2,1:T(8,128)(2,1)} %copy.75, bf16[8,32,2048]{1,0,2:T(8,128)(2,1)} %copy.71), kind=kOutput, calls=%fused_computation.23 | convolution fusion | flops 17039360 | bytes 5242880 | tf_op jit(solution)/shard_map/bsc,sch->bch/dot_general | solution.py:25
  179.2 5.1 copy.81
  184.3 6.9 %while.30 = (s32[]{:T(128)}, f32[2048,16]{0,1:T(8,128)S(1)}, f32[2048,16]{0,1:T(8,128)S(1)}, f32[8,2048,16]{1,2,0:T(8,128)}, f32[8,2048,16]{1,2,0:T(8,128)}, /*i...) while((s32[]{:T(128)}, f32[2048,16]{0,1:T(8,128)S(1)}, ...), condition=%wide.region_2.3_spmd.clone, body=%wide.region_1.2_spmd.clone.sunk | while | flops 393219 | bytes 1573500 | solution.py:61
  194.7 13.1 %copy.86 = f32[32,2048,16]{0,2,1:T(8,128)} copy(f32[32,2048,16]{1,2,0:T(8,128)} %get-tuple-element.286) | data formatting | bytes 8388608 | tf_op jit(solution)/shard_map/sub | solution.py:18
  207.8 6.8 %gather_fusion = f32[1024,2048]{1,0:T(8,128)} fusion(f32[32,2048]{1,0:T(8,128)S(1)} %get-tuple-element.285, s32[1024]{0:T(1024)S(1)} %broadcast_clamp_fusion), kind=kCustom, calls=%fused_computation | custom fusion | bytes 16781312 | tf_op jit(solution)/shard_map/gather | solution.py:44
  214.6 26.3 %copy.70 = f32[32,32,2048]{1,0,2:T(8,128)} copy(f32[32,32,2048]{2,1,0:T(8,128)} %bitcast.73) | data formatting | bytes 16777216 | tf_op jit(solution)/shard_map/gather | solution.py:44
  240.9 13.0 %copy.88 = f32[32,2048,16]{0,2,1:T(8,128)} copy(f32[32,2048,16]{1,2,0:T(8,128)} %get-tuple-element.287) | data formatting | bytes 8388608 | tf_op jit(solution)/shard_map/add | solution.py:18
  253.9 22.2 %fusion.4 = f32[2048,32,8]{1,2,0:T(8,128)} fusion(bf16[8,32,2048]{1,0,2:T(8,128)(2,1)} %copy.71, f32[32,32,2048]{1,0,2:T(8,128)} %copy.70, pred[32,32]{1,0:T(8,128)(4,1)S(1)} %bitcast.79), kind=kOutput, calls=%fused_computation.15 | convolution fusion | flops 35651584 | bytes 11535360 | tf_op jit(solution)/shard_map/bsc,tsc->btc/dot_general | solution.py:24
  276.1 18.8 %fusion.5 = f32[2048,32,8]{1,2,0:T(8,128)} fusion(bf16[8,32,2048]{1,0,2:T(8,128)(2,1)S(1)} %copy-done, f32[32,32,2048]{1,0,2:T(8,128)} %copy.70, pred[32,32]{1,0:T(8,128)(4,1)S(1)} %bitcast.80), kind=kOutput, calls=%fused_computation.16 | convolution fusion | flops 44040192 | bytes 11535360 | tf_op jit(solution)/shard_map/bsc,tsc->btc/dot_general | solution.py:25
  298.9 2.6 copy.94
  301.5 44.0 %while.31 = (s32[]{:T(128)}, f32[2048,16]{0,1:T(8,128)S(1)}, f32[2048,16]{0,1:T(8,128)S(1)}, s32[16]{0:T(128)S(1)}, s32[]{:T(128)}, /*index=5*/f32[2048,16]{0,1:...) while((s32[]{:T(128)}, f32[2048,16]{0,1:T(8,128)S(1)}, ...), condition=%wide.region_4.5_spmd.clone, body=%wide.region_3.4_spmd.clone.sunk | while | flops 393220 | bytes 1573009 | solution.py:90
  301.5 1.4 constant_dynamic-slice_fusion.3
  304.3 1.4 constant_dynamic-slice_fusion.3
  307.0 1.4 constant_dynamic-slice_fusion.3
  309.7 1.4 constant_dynamic-slice_fusion.3
  312.5 1.4 constant_dynamic-slice_fusion.3
  315.2 1.5 constant_dynamic-slice_fusion.3
  318.1 1.4 constant_dynamic-slice_fusion.3
  320.8 1.4 constant_dynamic-slice_fusion.3
  323.6 1.4 constant_dynamic-slice_fusion.3
  326.3 1.4 constant_dynamic-slice_fusion.3
  329.0 1.4 constant_dynamic-slice_fusion.3
  331.8 1.4 constant_dynamic-slice_fusion.3
  340.0 1.4 constant_dynamic-slice_fusion.3
  342.7 1.4 constant_dynamic-slice_fusion.3
  345.5 5.7 add_add_fusion
  351.2 4.6 copy.85
  355.8 5.4 copy.87
  361.2 18.5 %fusion.36 = f32[2048,8,32]{2,1,0:T(8,128)S(1)} fusion(f32[8,2048,16]{2,0,1:T(8,128)} %copy.85, f32[32,2048,16]{0,2,1:T(8,128)} %copy.86), kind=kOutput, calls=%fused_computation.85 | convolution fusion | flops 100663296 | bytes 7340032 | tf_op jit(solution)/shard_map/jch,bch->bjc/dot_general | solution.py:98
  379.8 21.9 %bitcast_add_fusion.2 = f32[8,32,2048]{1,0,2:T(8,128)} fusion(f32[2048,8,32]{2,1,0:T(8,128)S(1)} %fusion.36, f32[2048,32,8]{1,2,0:T(8,128)} %fusion.4, f32[2048,32,8]{1,2,0:T(8,128)} %fusion.5, f32[8,2048,16]{2,0,1:T(8,128)} %copy.87, f32[32,2048,16]{0,2,1:T(8,128)} %copy.88), kind=kOutput, calls=%fused_computation.21 | convolution fusion | flops 102236160 | bytes 13631488 | tf_op jit(solution)/shard_map/jch,bch->bjc/dot_general | solution.py:98
  401.6 5.5 copy.89
  407.1 1.6 bitcast_add_fusion.3
  408.8 25.1 %all-gather.11.cloned.1.call-done = bf16[4096,2048]{1,0:T(8,128)(2,1)} async-done(((bf16[256,2048]{1,0:T(8,128)(2,1)}), bf16[4096,2048]{1,0:T(8,128)(2,1)}) %all-gather.11.cloned.1.call-update) | async-done | bytes 16777232 | tf_op jit(solution)/shard_map/all_gather | solution.py:106
  433.9 12.9 %fusion.29 = bf16[256,2048]{1,0:T(8,128)(2,1)} fusion(bf16[256,4096]{1,0:T(8,128)(2,1)} %all-gather.9.cloned.1.call-done, bf16[4096,2048]{1,0:T(8,128)(2,1)} %all-gather.11.cloned.1.call-done, f32[256,2048]{1,0:T(8,128)} %bitcast_add_fusion.3), kind=kOutput, calls=%fused_computation.56 | convolution fusion | flops 4299685888 | bytes 22020096 | tf_op jit(solution)/shard_map/dot_general | solution.py:104
  446.8 113.7 %all-gather.15.cloned.1.call-done = bf16[4096,2048]{1,0:T(8,128)(2,1)} async-done(((bf16[256,2048]{1,0:T(8,128)(2,1)}), bf16[4096,2048]{1,0:T(8,128)(2,1)}) %all-gather.15.cloned.1.call-update) | async-done | bytes 16777232 | tf_op jit(solution)/shard_map/all_gather | solution.py:114
  560.5 32.7 %all-gather.13.cloned.1.call-done = bf16[256,4096]{1,0:T(8,128)(2,1)} async-done(((bf16[256,2048]{1,0:T(8,128)(2,1)}), bf16[256,4096]{1,0:T(8,128)(2,1)}) %all-gather.13.cloned.1.call-update) | async-done | bytes 2097168 | tf_op jit(solution)/shard_map/all_gather | solution.py:110
  593.2 11.9 %convolution_convert_fusion = bf16[256,2048]{1,0:T(8,128)(2,1)} fusion(bf16[256,4096]{1,0:T(8,128)(2,1)} %all-gather.13.cloned.1.call-done, bf16[4096,2048]{1,0:T(8,128)(2,1)} %all-gather.15.cloned.1.call-done), kind=kOutput, calls=%fused_computation.57 | convolution fusion | flops 4295491584 | bytes 19922944 | tf_op jit(solution)/shard_map/dot_general | solution.py:112
  (96 shorter events, 29.5 us)
Async XLA Ops:
  6.5 288.4 %all-gather.17.cloned.1.call-start = ((), (), s32[]{:S(2)}) async-start(), calls=%async_computation.4 | async-start | bytes 1114112 | tf_op jit(solution)/shard_map/all_gather | solution.py:68
  63.8 13.0 %copy-start.1 = (bf16[256,2048]{1,0:T(8,128)(2,1)S(1)}, bf16[256,2048]{1,0:T(8,128)(2,1)}, u32[]{:S(2)}) copy-start(bf16[256,2048]{1,0:T(8,128)(2,1)} %param.15) | copy-start | bytes 3145732
  191.9 105.6 %all-gather.19.cloned.1.call-start = ((), (), s32[]{:S(2)}) async-start(), calls=%async_computation.5 | async-start | bytes 1114112 | tf_op jit(solution)/shard_map/all_gather | solution.py:71
  192.7 216.1 %all-gather.9.cloned.1.call-start = ((), (), s32[]{:S(2)}) async-start(), calls=%async_computation | async-start | bytes 3145728 | tf_op jit(solution)/shard_map/all_gather | solution.py:102
  193.4 240.5 %all-gather.11.cloned.1.call-start = ((), (), s32[]{:S(2)}) async-start(), calls=%async_computation.1 | async-start | bytes 17825792 | tf_op jit(solution)/shard_map/all_gather | solution.py:106
  194.0 366.5 %all-gather.15.cloned.1.call-start = ((), (), s32[]{:S(2)}) async-start(), calls=%async_computation.3 | async-start | bytes 17825792 | tf_op jit(solution)/shard_map/all_gather | solution.py:114
  194.6 398.6 %all-gather.13.cloned.1.call-start = ((), (), s32[]{:S(2)}) async-start(), calls=%async_computation.2 | async-start | bytes 3145728 | tf_op jit(solution)/shard_map/all_gather | solution.py:110
  194.7 13.1 %copy-start.6 = (s32[1024]{0:T(1024)S(1)}, s32[1024]{0:T(1024)}, u32[]{:S(2)}) copy-start(s32[1024]{0:T(1024)} %constant.56) | copy-start | bytes 12292
  240.9 13.0 %copy-start.4 = (pred[32,32]{1,0:T(32,128)(4,1)S(1)}, pred[32,32]{1,0:T(32,128)(4,1)}, u32[]{:S(2)}) copy-start(pred[32,32]{1,0:T(32,128)(4,1)} %constant.52.clone) | copy-start | bytes 3076
  253.9 22.2 %copy-start = (bf16[8,32,2048]{1,0,2:T(8,128)(2,1)S(1)}, bf16[8,32,2048]{1,0,2:T(8,128)(2,1)}, u32[]{:S(2)}) copy-start(bf16[8,32,2048]{1,0,2:T(8,128)(2,1)} %copy.71) | copy-start | bytes 3145732
  301.5 44.0 %copy-start.3 = (f32[2048,16]{0,1:T(8,128)S(1)}, f32[2048,16]{0,1:T(8,128)}, u32[]{:S(2)}) copy-start(f32[2048,16]{0,1:T(8,128)} %param.17) | copy-start | bytes 393220
  401.6 5.5 copy-start.2
  401.6 5.5 copy-start.5
Sparse Core Ops, SparseCore 0:
  192.0 40.5 all-gather.16
  234.9 36.8 all-gather.18
  273.3 32.0 all-gather.8
  307.4 126.4 all-gather.10
  435.9 124.5 all-gather.14
  561.9 31.2 all-gather.12
where the time goes:
time: 621 us; the launch traced here: 612 us
  local copies, waits for them, and re-layouts  178 us (29%)
  waiting for transfers between devices  173 us (28%)
  matrix products  160 us (26%)
  other arithmetic  76.6 us (12%)
  between operations  14.1 us (2%)
  loops' own time  9.63 us (2%)
    all_gather x1, waiting for transfers between devices, per_device(): lax.all_gather(out_weight, 'seq', axis=0, tiled=True)  114 us
    convert_element_type x1, other arithmetic, split_einsum(): lower = (table - upper.astype(jnp.float32)).astype(jnp.bfloat16)  54.2 us
    dot_general x3, matrix products, split_einsum(): jnp.einsum(form, data, lower, preferred_element_type=jnp.float32)  48.3 us
    dot_general x3, matrix products, split_einsum(): first = jnp.einsum(form, data, upper, preferred_element_type=jnp.float32)  46.7 us
    gather x2, local copies, waits for them, and re-layouts, per_device(): toeplitz = jnp.where(causal[:, :, None], kernel[lag_index], 0.0)  33.1 us
    all_gather x1, waiting for transfers between devices, per_device(): hidden_all = lax.all_gather(hidden, 'tp', axis=1, tiled=True)  32.7 us
    dynamic_slice x32, local copies, waits for them, and re-layouts, per_device(): lax.scan(horner, (empty_state, empty_state), (counts, all_re, all_im))  32.2 us
    convert_element_type x2, local copies, waits for them, and re-layouts, split_einsum(): upper = table.astype(jnp.bfloat16)  26.2 us
  transfers between devices with their start and end apart: 6, of which 3 were waited for; matrix products, arithmetic and copies ran while one was open for 36% of the time, Pallas kernels for 0%

commit v1 on v0

v1 whole, which is shorter than its diff:
```python
import jax
import jax.numpy as jnp
from jax import lax
from jax.experimental import pallas as pl
from jax.experimental.pallas import tpu as pltpu
from jax.sharding import PartitionSpec as P

LANES = 128
UNROLL = 8
PIECE_BYTES = 512 * 1024


def small_gather(array, name, axis, split_axis):
    count = lax.axis_size(name)
    total = array.size * array.dtype.itemsize * count
    pieces = max(1, total // PIECE_BYTES)
    while array.shape[split_axis] % pieces:
        pieces -= 1
    parts = jnp.split(array, pieces, axis=split_axis)
    done = [lax.all_gather(part, name, axis=axis, tiled=True) for part in parts]
    return done[0] if pieces == 1 else jnp.concatenate(done, axis=split_axis)


def step_state(state, values, q_re, q_im):
    advanced = []
    for (re, im), a, b in zip(state, q_re, q_im):
        advanced.append((a * re - b * im + values, a * im + b * re))
    return advanced


def end_kernel(x_ref, q_re_ref, q_im_ref, end_re_ref, end_im_ref):
    dims = q_re_ref.shape[0]
    q_re = [q_re_ref[h] for h in range(dims)]
    q_im = [q_im_ref[h] for h in range(dims)]
    zero = jnp.zeros(q_re[0].shape, jnp.float32)

    def body(i, state):
        for u in range(UNROLL):
            state = step_state(state, x_ref[i * UNROLL + u], q_re, q_im)
        return state

    state = lax.fori_loop(0, x_ref.shape[0] // UNROLL, body, [(zero, zero)] * dims)
    for h in range(dims):
        end_re_ref[h] = state[h][0]
        end_im_ref[h] = state[h][1]


def smooth_kernel(
    position_ref, x_ref, q_re_ref, q_im_ref, c_re_ref, c_im_ref, span_re_ref, span_im_ref,
    ends_re_ref, ends_im_ref, skip_ref, y_ref,
):
    dims = q_re_ref.shape[0]
    zero = jnp.zeros(q_re_ref.shape[1:], jnp.float32)

    def horner(k, state):
        moved = []
        for h in range(dims):
            re, im = state[h]
            a, b = span_re_ref[h], span_im_ref[h]
            moved.append((
                a * re - b * im + ends_re_ref[k, h].astype(jnp.float32),
                a * im + b * re + ends_im_ref[k, h].astype(jnp.float32),
            ))
        return moved

    state = lax.fori_loop(0, position_ref[0], horner, [(zero, zero)] * dims)
    q_re = [q_re_ref[h] for h in range(dims)]
    q_im = [q_im_ref[h] for h in range(dims)]
    c_re = [c_re_ref[h] for h in range(dims)]
    c_im = [c_im_ref[h] for h in range(dims)]

    @pl.when(pl.program_id(1) == 0)
    def _():
        y_ref[...] = x_ref[...] * skip_ref[...][None]

    def body(i, state):
        for u in range(UNROLL):
            t = i * UNROLL + u
            state = step_state(state, x_ref[t], q_re, q_im)
            sums = [c_re[h] * state[h][0] - c_im[h] * state[h][1] for h in range(dims)]
            while len(sums) > 1:
                sums = [sum(sums[k:k + 2]) for k in range(0, len(sums), 2)]
            y_ref[t] += sums[0]
        return state

    lax.fori_loop(0, x_ref.shape[0] // UNROLL, body, state)


def per_device(tokens, decay_rate, angle, in_coef, out_coef, skip_coef, gate_weight, out_weight):
    rows, channels = tokens.shape
    dims = decay_rate.shape[1]
    tiles = channels // LANES
    sub = 8 if tiles % 8 == 0 else tiles
    half = dims // 2 if dims % 2 == 0 else dims
    grid = (tiles // sub, dims // half)

    gate_all = lax.all_gather(gate_weight, "seq", axis=0, tiled=True)
    out_all = lax.all_gather(out_weight, "seq", axis=0, tiled=True)

    def spread(table):
        return table.T.reshape(dims, tiles, LANES)

    rate = spread(decay_rate)
    theta = spread(angle)
    magnitude = 1.0 - rate
    scaled = spread(in_coef) * jnp.sqrt(1.0 - magnitude * magnitude)
    c_re = scaled * spread(out_coef[0])
    c_im = scaled * spread(out_coef[1])
    q_re = magnitude * jnp.cos(theta)
    q_im = magnitude * jnp.sin(theta)
    span_mag = jnp.exp(rows * jnp.log1p(-rate))
    span_re = span_mag * jnp.cos(rows * theta)
    span_im = span_mag * jnp.sin(rows * theta)
    values = tokens.astype(jnp.float32).reshape(rows, tiles, LANES)

    x_spec = pl.BlockSpec((rows, sub, LANES), lambda g, h: (0, g, 0))
    table_spec = pl.BlockSpec((half, sub, LANES), lambda g, h: (h, g, 0))
    table_shape = jax.ShapeDtypeStruct((dims, tiles, LANES), jnp.float32)
    end_re, end_im = pl.pallas_call(
        end_kernel,
        grid=grid,
        in_specs=[x_spec, table_spec, table_spec],
        out_specs=[table_spec, table_spec],
        out_shape=[table_shape, table_shape],
        name="end_state",
    )(values, q_re, q_im)

    columns = small_gather(tokens, "tp", 1, 0)
    ends_re = small_gather(end_re.astype(jnp.bfloat16)[None], "seq", 0, 1)
    ends_im = small_gather(end_im.astype(jnp.bfloat16)[None], "seq", 0, 1)
    devices = ends_re.shape[0]
    ends_spec = pl.BlockSpec((devices, half, sub, LANES), lambda g, h: (0, h, g, 0))
    position = lax.axis_index("seq").astype(jnp.int32).reshape(1)
    smoothed = pl.pallas_call(
        smooth_kernel,
        grid=grid,
        in_specs=[pl.BlockSpec(memory_space=pltpu.SMEM), x_spec]
        + [table_spec] * 6
        + [ends_spec, ends_spec, pl.BlockSpec((sub, LANES), lambda g, h: (g, 0))],
        out_specs=x_spec,
        out_shape=jax.ShapeDtypeStruct((rows, tiles, LANES), jnp.float32),
        name="smooth",
    )(
        position, values, q_re, q_im, c_re, c_im, span_re, span_im, ends_re, ends_im,
        skip_coef.reshape(tiles, LANES),
    ).reshape(rows, channels)
    activated = jax.nn.silu(smoothed)
    gate_pre = jnp.dot(columns, gate_all, preferred_element_type=jnp.float32)
    hidden = (activated * jax.nn.sigmoid(gate_pre)).astype(jnp.bfloat16)
    hidden_all = small_gather(hidden, "tp", 1, 0)
    mixed_out = jnp.dot(hidden_all, out_all, preferred_element_type=jnp.float32)
    return mixed_out.astype(jnp.bfloat16)


def solution(mesh):
    in_specs = (
        P("seq", "tp"),
        P("tp", None),
        P("tp", None),
        P("tp", None),
        P(None, "tp", None),
        P("tp"),
        P("seq", "tp"),
        P("seq", "tp"),
    )
    return jax.shard_map(
        per_device, mesh=mesh, in_specs=in_specs, out_specs=P("seq", "tp"), check_vma=False
    )
```

time: 621 us -> 296 us (0.48); the launches traced: 612 us -> 296 us
  local copies, waits for them, and re-layouts: 178 us -> 5.88 us
  blocking collectives: 0 us -> 160 us
  matrix products: 160 us -> 20.6 us
  waiting for transfers between devices: 173 us -> 66.3 us
  other arithmetic: 76.6 us -> 4.47 us
  Pallas kernels: 0 us -> 25.4 us
  loops' own time: 9.63 us -> 0 us
    all_gather x0 -> x12, blocking collectives: none -> 160 us  [small_gather(): done = [lax.all_gather(part, name, axis=axis, tiled=True) for part in parts]]
    dot_general x10 -> x2, matrix products: 160 us -> 20.6 us  [the longest x1 11.4 us: per_device(): gate_pre = jnp.dot(columns, gate_all, preferred_element_type=jnp.float32)]
    all_gather x6 -> x2, waiting for transfers between devices: 171 us -> 65 us  [the longest x1 65 us: per_device(): out_all = lax.all_gather(out_weight, 'seq', axis=0, tiled=True)]
    convert_element_type x6 -> x0, other arithmetic: 58.2 us -> none  [the longest x1 54.2 us: split_einsum(): lower = (table - upper.astype(jnp.float32)).astype(jnp.bfloat16)]
    convert_element_type x4 -> x0, local copies, waits for them, and re-layouts: 52 us -> none  [the longest x2 26.2 us: split_einsum(): upper = table.astype(jnp.bfloat16)]
    gather x2 -> x0, local copies, waits for them, and re-layouts: 33.1 us -> none  [per_device(): toeplitz = jnp.where(causal[:, :, None], kernel[lag_index], 0.0)]
    dynamic_slice x32 -> x0, local copies, waits for them, and re-layouts: 32.2 us -> none  [per_device(): lax.scan(horner, (empty_state, empty_state), (counts, all_re, all_im))]
    add x4 -> x0, local copies, waits for them, and re-layouts: 28.5 us -> none  [the longest x1 13 us: complex_mul(): left_re * right_im + left_im * right_re]
  transfers between devices with their start and end apart: 6 -> 2, of which waited for: 3 -> 1; matrix products, arithmetic and copies ran while one was open for 36% -> 7% of each run, Pallas kernels for 0% -> 9%
where the time goes in v1:
time: 296 us
  blocking collectives  160 us (54%)
  waiting for transfers between devices  66.3 us (22%)
  Pallas kernels  25.4 us (9%)
  matrix products  20.6 us (7%)
  between operations  13.5 us (5%)
  local copies, waits for them, and re-layouts  5.88 us (2%)
  other arithmetic  4.47 us (2%)
    all_gather x12, blocking collectives, small_gather(): done = [lax.all_gather(part, name, axis=axis, tiled=True) for part in parts]  160 us
    all_gather x1, waiting for transfers between devices, per_device(): out_all = lax.all_gather(out_weight, 'seq', axis=0, tiled=True)  65 us
    pallas_call x1, Pallas kernels, per_device(): pl.pallas_call(smooth_kernel, grid=grid, in_specs=[pl.BlockSpec(memory_sp...  15.4 us
    dot_general x1, matrix products, per_device(): gate_pre = jnp.dot(columns, gate_all, preferred_element_type=jnp.float32)  11.4 us
    pallas_call x1, Pallas kernels, per_device(): pl.pallas_call(end_kernel, grid=grid, in_specs=[x_spec, table_spec, table...  9.97 us
    dot_general x1, matrix products, per_device(): mixed_out = jnp.dot(hidden_all, out_all, preferred_element_type=jnp.float32)  9.2 us
  transfers between devices with their start and end apart: 2, of which 1 were waited for; matrix products, arithmetic and copies ran while one was open for 7% of the time, Pallas kernels for 9%

profile of v1, /device:TPU:0, one launch (start us, length us, event | category | flops | bytes accessed | tf_op | source)
XLA Modules:
  0.0 295.9 jit_solution(1825525083746880362)
XLA Ops:
  6.5 0.0 copy-start.3
  6.5 0.0 copy-start.5
  6.5 0.0 copy-start.2
  6.5 0.0 copy-start.4
  6.5 0.0 copy-start
  6.5 0.0 all-gather.3.cloned.1.call-start
  6.6 0.7 all-gather.3.cloned.1.call-update
  7.3 0.0 all-gather.5.cloned.1.call-start
  7.3 0.7 all-gather.5.cloned.1.call-update
  8.0 0.0 copy-done.3
  8.0 0.0 copy-done.5
  8.1 0.0 copy-done.2
  8.1 0.0 copy-done.4
  8.1 1.1 multiply_bitcast_fusion
  9.2 0.7 copy.10
  9.9 0.7 copy.11
  10.5 0.0 copy-done
  10.5 0.2 convert_bitcast_fusion
  10.8 1.7 copy.9
  12.5 0.7 copy.12
  13.1 0.7 copy.13
  13.8 0.7 copy.14
  14.5 0.7 copy.15
  15.1 10.0 %end_state.1 = (f32[16,16,128]{2,1,0:T(8,128)}, f32[16,16,128]{2,1,0:T(8,128)}) custom-call(f32[256,16,128]{2,1,0:T(8,128)} %bitcast.57, f32[16,16,128]{2,1,0:T(8,128)} %bitcast.60, f32[16,16,128]{2,1,0:T(8,128)} %bitcast.62), custom_call_target="tpu_custom_call" | custom-call | tf_op jit(solution)/shard_map/end_state/pallas_call | solution.py:119
  25.1 1.0 convert_bitcast_fusion.1
  26.1 27.9 %all_gather.44 = bf16[16,8,16,128]{3,2,1,0:T(8,128)(2,1)S(1)} all-gather(bf16[1,8,16,128]{3,2,1,0:T(8,128)(2,1)S(1)} %get-tuple-element.25), channel_id=1, replica_groups=mesh['seq'=16,'tp'=2] {'seq'}, dimensions={0}, use_global_device_ids=true | all-gather | bytes 557056 | tf_op jit(solution)/shard_map/all_gather | solution.py:20
  54.0 20.6 %all_gather.45 = bf16[16,8,16,128]{3,2,1,0:T(8,128)(2,1)S(1)} all-gather(bf16[1,8,16,128]{3,2,1,0:T(8,128)(2,1)S(1)} %get-tuple-element.26), channel_id=1, replica_groups=mesh['seq'=16,'tp'=2] {'seq'}, dimensions={0}, use_global_device_ids=true | all-gather | bytes 557056 | tf_op jit(solution)/shard_map/all_gather | solution.py:20
  74.6 1.1 pad_maximum_fusion.1.ends_im_ref
  75.7 24.5 %all_gather.42 = bf16[16,8,16,128]{3,2,1,0:T(8,128)(2,1)S(1)} all-gather(bf16[1,8,16,128]{3,2,1,0:T(8,128)(2,1)S(1)} %get-tuple-element.27), channel_id=1, replica_groups=mesh['seq'=16,'tp'=2] {'seq'}, dimensions={0}, use_global_device_ids=true | all-gather | bytes 557056 | tf_op jit(solution)/shard_map/all_gather | solution.py:20
  100.2 21.8 %all_gather.43 = bf16[16,8,16,128]{3,2,1,0:T(8,128)(2,1)S(1)} all-gather(bf16[1,8,16,128]{3,2,1,0:T(8,128)(2,1)S(1)} %get-tuple-element.28), channel_id=1, replica_groups=mesh['seq'=16,'tp'=2] {'seq'}, dimensions={0}, use_global_device_ids=true | all-gather | bytes 557056 | tf_op jit(solution)/shard_map/all_gather | solution.py:20
  122.1 1.1 pad_maximum_fusion.ends_re_ref
  123.2 15.4 %smooth.1 = f32[256,16,128]{2,1,0:T(8,128)} custom-call(s32[1]{0:T(128)} %bitcast.position_ref, f32[256,16,128]{2,1,0:T(8,128)} %bitcast.58, f32[16,16,128]{2,1,0:T(8,128)} %bitcast.61, f32[16,16,128]{2,1,0:T(8,128)} %bitcast.63, f32[16,16,128]{2,1,0:T(8,128)} %bitcast.64, f32[16,16,128]{2,1,0:T(8,128)} %bitcast.65, f32[16,16,128]{2,1,0:T(8,128)} %bitcast.66, ...), custom_call_target="tpu_custom_call" | custom-call | tf_op jit(solution)/shard_map/smooth/pallas_call | solution.py:134
  138.6 0.1 fusion.27
  138.6 0.0 copy-start.1
  138.7 9.4 %all_gather.46 = bf16[64,4096]{1,0:T(8,128)(2,1)S(1)} all-gather(bf16[64,2048]{1,0:T(8,128)(2,1)S(1)} %get-tuple-element.13), channel_id=1, replica_groups=mesh['seq'=16,'tp'=2] {'tp'}, dimensions={1}, use_global_device_ids=true | all-gather | bytes 786432 | tf_op jit(solution)/shard_map/all_gather | solution.py:20
  148.1 8.5 %all_gather.47 = bf16[64,4096]{1,0:T(8,128)(2,1)S(1)} all-gather(bf16[64,2048]{1,0:T(8,128)(2,1)S(1)} %get-tuple-element.14), channel_id=1, replica_groups=mesh['seq'=16,'tp'=2] {'tp'}, dimensions={1}, use_global_device_ids=true | all-gather | bytes 786432 | tf_op jit(solution)/shard_map/all_gather | solution.py:20
  156.6 7.8 %all_gather.48 = bf16[64,4096]{1,0:T(8,128)(2,1)} all-gather(bf16[64,2048]{1,0:T(8,128)(2,1)S(1)} %get-tuple-element.16), channel_id=1, replica_groups=mesh['seq'=16,'tp'=2] {'tp'}, dimensions={1}, use_global_device_ids=true | all-gather | bytes 786432 | tf_op jit(solution)/shard_map/all_gather | solution.py:20
  164.3 7.1 %all_gather.49 = bf16[64,4096]{1,0:T(8,128)(2,1)} all-gather(bf16[64,2048]{1,0:T(8,128)(2,1)S(1)} %get-tuple-element.15), channel_id=1, replica_groups=mesh['seq'=16,'tp'=2] {'tp'}, dimensions={1}, use_global_device_ids=true | all-gather | bytes 786432 | tf_op jit(solution)/shard_map/all_gather | solution.py:20
  171.5 0.0 all-gather.3.cloned.1.call-done
  171.5 0.0 copy-done.1
  171.5 11.4 %fusion.4 = bf16[256,2048]{1,0:T(8,128)(2,1)S(1)} fusion(bf16[4096,2048]{1,0:T(8,128)(2,1)} %all-gather.3.cloned.1.call-done, f32[32,8,16,128]{3,2,1,0:T(8,128)S(1)} %bitcast.59, bf16[64,4096]{1,0:T(8,128)(2,1)} %all_gather.49, bf16[64,4096]{1,0:T(8,128)(2,1)} %all_gather.48, bf16[64,4096]{1,0:T(8,128)(2,1)S(1)} %all_gather.47, ...), kind=kOutput, calls=%fused_computation.5 | convolution fusion | flops 4308074496 | bytes 22020096 | tf_op jit(solution)/shard_map/dot_general | solution.py:148
  182.9 0.1 fusion.26
  183.0 7.5 %all_gather.51 = bf16[64,4096]{1,0:T(8,128)(2,1)S(1)} all-gather(bf16[64,2048]{1,0:T(8,128)(2,1)S(1)} %get-tuple-element.9), channel_id=1, replica_groups=mesh['seq'=16,'tp'=2] {'tp'}, dimensions={1}, use_global_device_ids=true | all-gather | bytes 786432 | tf_op jit(solution)/shard_map/all_gather | solution.py:20
  190.4 8.2 %all_gather.52 = bf16[64,4096]{1,0:T(8,128)(2,1)S(1)} all-gather(bf16[64,2048]{1,0:T(8,128)(2,1)S(1)} %get-tuple-element.12), channel_id=1, replica_groups=mesh['seq'=16,'tp'=2] {'tp'}, dimensions={1}, use_global_device_ids=true | all-gather | bytes 786432 | tf_op jit(solution)/shard_map/all_gather | solution.py:20
  198.7 9.2 %all_gather.53 = bf16[64,4096]{1,0:T(8,128)(2,1)S(1)} all-gather(bf16[64,2048]{1,0:T(8,128)(2,1)S(1)} %get-tuple-element.11), channel_id=1, replica_groups=mesh['seq'=16,'tp'=2] {'tp'}, dimensions={1}, use_global_device_ids=true | all-gather | bytes 786432 | tf_op jit(solution)/shard_map/all_gather | solution.py:20
  207.8 7.0 %all_gather.54 = bf16[64,4096]{1,0:T(8,128)(2,1)S(1)} all-gather(bf16[64,2048]{1,0:T(8,128)(2,1)S(1)} %get-tuple-element.10), channel_id=1, replica_groups=mesh['seq'=16,'tp'=2] {'tp'}, dimensions={1}, use_global_device_ids=true | all-gather | bytes 786432 | tf_op jit(solution)/shard_map/all_gather | solution.py:20
  214.9 65.0 %all-gather.5.cloned.1.call-done = bf16[4096,2048]{1,0:T(8,128)(2,1)} async-done(((bf16[256,2048]{1,0:T(8,128)(2,1)}), bf16[4096,2048]{1,0:T(8,128)(2,1)}) %all-gather.5.cloned.1.call-update) | async-done | bytes 16777232 | tf_op jit(solution)/shard_map/all_gather | solution.py:98
  279.8 9.2 %convolution_convert_fusion = bf16[256,2048]{1,0:T(8,128)(2,1)} fusion(bf16[4096,2048]{1,0:T(8,128)(2,1)} %all-gather.5.cloned.1.call-done, bf16[64,4096]{1,0:T(8,128)(2,1)S(1)} %all_gather.54, bf16[64,4096]{1,0:T(8,128)(2,1)S(1)} %all_gather.53, bf16[64,4096]{1,0:T(8,128)(2,1)S(1)} %all_gather.52, bf16[64,4096]{1,0:T(8,128)(2,1)S(1)} %all_gather.51), kind=kOutput, calls=%fused_computation.6 | convolution fusion | flops 4303880192 | bytes 19922944 | tf_op jit(solution)/shard_map/dot_general | solution.py:151
  (2 shorter events, 0.0 us)
Async XLA Ops:
  6.5 1.5 copy-start.3
  6.5 1.5 copy-start.5
  6.5 1.5 copy-start.2
  6.5 1.5 copy-start.4
  6.5 4.0 %copy-start = (bf16[256,2048]{1,0:T(8,128)(2,1)S(1)}, bf16[256,2048]{1,0:T(8,128)(2,1)}, u32[]{:S(2)}) copy-start(bf16[256,2048]{1,0:T(8,128)(2,1)} %param.8) | copy-start | bytes 3145732
  6.5 164.9 %all-gather.3.cloned.1.call-start = ((), (), s32[]{:S(2)}) async-start(), calls=%async_computation | async-start | bytes 17825792 | tf_op jit(solution)/shard_map/all_gather | solution.py:97
  7.3 272.6 %all-gather.5.cloned.1.call-start = ((), (), s32[]{:S(2)}) async-start(), calls=%async_computation.1 | async-start | bytes 17825792 | tf_op jit(solution)/shard_map/all_gather | solution.py:98
  138.6 32.8 %copy-start.1 = (f32[256,16,128]{2,1,0:T(8,128)S(1)}, f32[256,16,128]{2,1,0:T(8,128)}, u32[]{:S(2)}) copy-start(f32[256,16,128]{2,1,0:T(8,128)} %smooth.1) | copy-start | bytes 6291460
Sparse Core Ops, SparseCore 0:
  9.5 143.1 all-gather.2
  154.9 124.9 all-gather.4
